TPU v7x, 256 devices: a 4x2x16 block of a 4x16x16 slice. The times are simulated.
256 devices in a mesh: groups: 2 (over y), row: 16 (over z), col: 4 (over x), sub: 2 (over core).
Axes of the slice: x: 4, y: 2, z: 16, core: 2. Of those that a mesh axis runs over, the one named last changes fastest.
The devices are a block of a 4x16x16 slice.
Arguments:
- saved_alignment: bfloat16 [64, 1024, 256], P(('col', 'sub'), ('groups', 'row')), parts along dimension 1, may hold values from -6 to 6
- homolog_existence: int32 [64, 1024], P(('col', 'sub'), ('groups', 'row')), parts along dimension 1, may hold values 0 or 1
- amino_existence: int32 [1024], P(('groups', 'row')), parts along dimension 0, may hold values 0 or 1
- couple_delta_adjoint: bfloat16 [1024, 512, 128], P(('groups', 'row'), ('col', 'sub')), parts along dimension 0, may hold values from -1.5 to 1.5
- feedforward_adjoint: bfloat16 [64, 1024, 256], P(('col', 'sub'), ('groups', 'row')), parts along dimension 1, may hold values from -1.5 to 1.5
- feedforward_scale: float32 [256], replicated, may hold values from 0.1 to 1.9
- expansion_matrix: bfloat16 [256, 1024], replicated, may hold values from -0.375 to 0.375
- contraction_matrix: bfloat16 [1024, 256], replicated, may hold values from -0.1875 to 0.1875
- product_scale_vector: float32 [256], replicated, may hold values from 0.1 to 1.9
- twin_operand_matrix: bfloat16 [256, 64], replicated, may hold values from -0.375 to 0.375
- couple_projection_matrix: bfloat16 [1024, 128], replicated, may hold values from -0.1875 to 0.1875
Outputs:
- alignment_start_adjoint: bfloat16 [64, 1024, 256], P(('col', 'sub'), ('groups', 'row')), parts along dimension 1
- grad_out_weight: float32 [2048, 128], P('groups'), parts along dimension 0
- grad_factor_weight: float32 [512, 64], P('groups'), parts along dimension 0
- grad_w_in: float32 [512, 1024], P('groups'), parts along dimension 0
- grad_w_mid: float32 [2048, 256], P('groups'), parts along dimension 0
- feedforward_scale_adjoint: float32 [512], P('groups'), parts along dimension 0
- product_scale_adjoint: float32 [512], P('groups'), parts along dimension 0
There are 2 independent parts, one for each index of `groups`. A program takes and returns all parts, laid end to end along the dimension named above; an argument that names none is the same for every part. Nothing has to cross between parts.
All inputs are finite; a program needn't handle non-finite values. No bound on the sum of `homolog_existence` or of `amino_existence` on one device may be relied on, other than what follows from the above.
Results may differ from a plain program's by a relative error of at most 0.015.
Values may be sent and summed in bfloat16 or wider, within the bound.
No kernel may reach another device: no remote copies, remote signals or barrier semaphores. Data moves between devices by JAX's collectives and lax.ppermute only.
A program may use at most 64 MiB of HBM per device.

v0:
```python
import math
import jax
import jax.numpy as jnp
from jax import lax
from jax.sharding import PartitionSpec as P

epsilon = 1e-05


def in_one_piece(arrays, axis, dim, along):
    ends, at = ([], 0)
    for a in arrays[:-1]:
        at += a.shape[along]
        ends.append(at)
    both = jnp.concatenate(arrays, axis=along)
    return tuple(jnp.split(lax.all_gather(both, axis, axis=dim, tiled=True), ends, axis=along))


def joined_along(parts, dim):
    parts = jnp.moveaxis(parts, 0, dim)
    lengths = parts.shape
    return parts.reshape(*lengths[:dim], lengths[dim] * lengths[dim + 1], *lengths[dim + 2 :])


def one_gather(arrays, axis, dims):
    vector = jnp.concatenate([a.reshape(-1) for a in arrays])
    lines, at, done = (lax.all_gather(vector, axis), 0, [])
    for a, dim in zip(arrays, dims):
        parts = lines[:, at : at + a.size].reshape(-1, *a.shape)
        done.append(joined_along(parts, dim))
        at += a.size
    return tuple(done)


def split_up(shard, dim, devices):
    lengths = shard.shape
    parts = shard.reshape(*lengths[:dim], devices, lengths[dim] // devices, *lengths[dim + 1 :])
    return jnp.moveaxis(parts, dim, 0)


def sent_and_summed(shard, axis, dim):
    parts = split_up(shard, dim, lax.axis_size(axis))
    arrived = lax.all_to_all(parts, axis, split_axis=0, concat_axis=0, tiled=True)
    return arrived.astype(jnp.float32).sum(axis=0)


def layer_normalize(values):
    centre = jnp.mean(values, axis=-1, keepdims=True)
    centred = values - centre
    variance = jnp.mean(centred * centred, axis=-1, keepdims=True)
    inv_std = lax.rsqrt(variance + epsilon)
    return (centred * inv_std, inv_std)


def standardizer_adjoint(grad_hat, normed, inv_std):
    first_mean = jnp.mean(grad_hat, axis=-1, keepdims=True)
    second_mean = jnp.mean(grad_hat * normed, axis=-1, keepdims=True)
    return inv_std * (grad_hat - first_mean - normed * second_mean)


def exact_gelu(values):
    return jax.nn.gelu(values, approximate=False)


def contract_rows(first_arr, second_arr):
    return lax.dot_general(
        first_arr, second_arr, (((0,), (0,)), ((), ())), preferred_element_type=jnp.float32
    )


def contract_last(first_arr, second_arr):
    return lax.dot_general(
        first_arr, second_arr, (((1,), (1,)), ((), ())), preferred_element_type=jnp.float32
    )


def per_device(
    saved_alignment,
    homolog_existence,
    amino_existence,
    couple_delta_adjoint,
    feedforward_adjoint,
    feedforward_scale,
    expansion_matrix,
    contraction_matrix,
    product_scale_vector,
    twin_operand_matrix,
    couple_projection_matrix,
):
    homolog_split_total, amino_split_total, lane_breadth = saved_alignment.shape
    factor = twin_operand_matrix.shape[1] // 2
    pair_width = couple_projection_matrix.shape[1]
    existing_record_lines = homolog_split_total * amino_split_total
    shard_count = lax.axis_size(("col", "sub"))
    row_devices = lax.axis_size("row")
    total_res = amino_split_total * row_devices
    col_res = total_res // shard_count
    all_seqs = homolog_split_total * shard_count
    embedding_numbers = saved_alignment.astype(jnp.float32).reshape(
        existing_record_lines, lane_breadth
    )
    transition_standardized, transition_inv_deviation = layer_normalize(embedding_numbers)
    normalized_input = (transition_standardized * feedforward_scale).astype(jnp.bfloat16)
    hidden_pre = jnp.dot(normalized_input, expansion_matrix, preferred_element_type=jnp.float32)
    gelu_value, gelu_back = jax.vjp(exact_gelu, hidden_pre)
    hidden = gelu_value.astype(jnp.bfloat16)
    mixed_values = embedding_numbers + jnp.dot(
        hidden, contraction_matrix, preferred_element_type=jnp.float32
    )
    product_zscored, product_reciprocal_spread = layer_normalize(mixed_values)
    normalized_output = (product_zscored * product_scale_vector).astype(jnp.bfloat16)
    projected = jnp.dot(normalized_output, twin_operand_matrix, preferred_element_type=jnp.float32)
    keep_mask = (homolog_existence * amino_existence[None, :]).astype(jnp.float32)
    keep_col = keep_mask.reshape(existing_record_lines, 1)
    left_factor = (
        (projected[:, :factor] * keep_col)
        .astype(jnp.bfloat16)
        .reshape(homolog_split_total, amino_split_total * factor)
    )
    right_factor = (
        (projected[:, factor:] * keep_col)
        .astype(jnp.bfloat16)
        .reshape(homolog_split_total, amino_split_total * factor)
    )
    keep_half = keep_mask.astype(jnp.bfloat16)
    left_all, keep_rows = in_one_piece((left_factor, keep_half), ("col", "sub"), 0, 1)
    right_spread, keep_spread = one_gather((right_factor, keep_half), "row", (1, 1))
    right_flat, keep_cols = (
        lax.all_to_all(right_spread, ("col", "sub"), split_axis=1, concat_axis=0, tiled=True),
        lax.all_to_all(keep_spread, ("col", "sub"), split_axis=1, concat_axis=0, tiled=True),
    )
    right_cols = right_flat.reshape(all_seqs, col_res, factor)
    left_rows = left_all.reshape(all_seqs, amino_split_total, factor)
    pair_count = contract_rows(keep_rows, keep_cols)
    inverse = 1.0 / jnp.maximum(pair_count, 1.0)
    block_rows = math.gcd(amino_split_total, 16)
    result_adjoint = jnp.zeros((factor * factor, pair_width), jnp.float32)
    grad_right = jnp.zeros((all_seqs, col_res, factor), jnp.float32)
    left_parts = []
    for row_start in range(0, amino_split_total, block_rows):
        left_block = left_rows[:, row_start : row_start + block_rows, :]
        inv_block = inverse[row_start : row_start + block_rows]
        cot_block = couple_delta_adjoint[row_start : row_start + block_rows]
        outer_sum = jnp.einsum(
            "sip,sjq->ijpq", left_block, right_cols, preferred_element_type=jnp.float32
        )
        outer_half = (outer_sum * inv_block[:, :, None, None]).astype(jnp.bfloat16)
        outer_half = outer_half.reshape(block_rows, col_res, factor * factor)
        result_adjoint = result_adjoint + jnp.einsum(
            "ijk,ijl->kl", outer_half, cot_block, preferred_element_type=jnp.float32
        )
        pair_back = jnp.einsum(
            "ijl,kl->ijk", cot_block, couple_projection_matrix, preferred_element_type=jnp.float32
        )
        back_half = (pair_back * inv_block[:, :, None]).astype(jnp.bfloat16)
        back_half = back_half.reshape(block_rows, col_res, factor, factor)
        left_parts.append(
            jnp.einsum("ijpq,sjq->sip", back_half, right_cols, preferred_element_type=jnp.float32)
        )
        grad_right = grad_right + jnp.einsum(
            "ijpq,sip->sjq", back_half, left_block, preferred_element_type=jnp.float32
        )
    grad_left = jnp.concatenate(left_parts, axis=1).reshape(all_seqs, amino_split_total * factor)
    left_own = sent_and_summed(grad_left.astype(jnp.bfloat16), ("col", "sub"), 0)
    right_back = lax.all_to_all(
        grad_right.reshape(all_seqs, col_res * factor).astype(jnp.bfloat16),
        ("col", "sub"),
        split_axis=0,
        concat_axis=1,
        tiled=True,
    )
    right_own = sent_and_summed(right_back, "row", 1)
    grad_proj = jnp.concatenate(
        [
            left_own.reshape(existing_record_lines, factor),
            right_own.reshape(existing_record_lines, factor),
        ],
        axis=1,
    )
    grad_proj = (grad_proj * keep_col).astype(jnp.bfloat16)
    operand_adjoint = contract_rows(normalized_output, grad_proj)
    rescaled_result_adjoint = contract_last(grad_proj, twin_operand_matrix)
    product_scale_adjoint = jnp.sum(rescaled_result_adjoint * product_zscored, axis=0)
    combined_adjoint = feedforward_adjoint.astype(jnp.float32).reshape(
        existing_record_lines, lane_breadth
    ) + standardizer_adjoint(
        rescaled_result_adjoint * product_scale_vector, product_zscored, product_reciprocal_spread
    )
    grad_mixed_half = combined_adjoint.astype(jnp.bfloat16)
    hidden_adjoint = contract_rows(hidden, grad_mixed_half)
    grad_hidden = contract_last(grad_mixed_half, contraction_matrix)
    grad_pre = gelu_back(grad_hidden)[0].astype(jnp.bfloat16)
    expansion_adjoint = contract_rows(normalized_input, grad_pre)
    normed_input_gradient = contract_last(grad_pre, expansion_matrix)
    feedforward_scale_adjoint = jnp.sum(normed_input_gradient * transition_standardized, axis=0)
    alignment_start_adjoint = combined_adjoint + standardizer_adjoint(
        normed_input_gradient * feedforward_scale, transition_standardized, transition_inv_deviation
    )
    weight_grads = lax.psum(
        (
            result_adjoint,
            operand_adjoint,
            expansion_adjoint,
            hidden_adjoint,
            feedforward_scale_adjoint,
            product_scale_adjoint,
        ),
        ("row", "col", "sub"),
    )
    return (
        alignment_start_adjoint.astype(jnp.bfloat16).reshape(
            homolog_split_total, amino_split_total, lane_breadth
        ),
        weight_grads[0],
        weight_grads[1],
        weight_grads[2],
        weight_grads[3],
        weight_grads[4],
        weight_grads[5],
    )


def solution(mesh):
    return jax.shard_map(
        per_device,
        mesh=mesh,
        in_specs=(
            P(("col", "sub"), ("groups", "row"), None),
            P(("col", "sub"), ("groups", "row")),
            P(("groups", "row")),
            P(("groups", "row"), ("col", "sub"), None),
            P(("col", "sub"), ("groups", "row"), None),
            P(),
            P(),
            P(),
            P(),
            P(),
            P(),
        ),
        out_specs=(
            P(("col", "sub"), ("groups", "row"), None),
            P("groups", None),
            P("groups", None),
            P("groups", None),
            P("groups", None),
            P("groups"),
            P("groups"),
        ),
        check_vma=False,
    )
```

profile of v0, /device:TPU:33, one launch (start us, length us, event | category | flops | bytes accessed | tf_op | source)
XLA Modules:
  0.0 527.1 jit_solution(18394093957308587515)
XLA Ops:
  7.2 1.1 convert_reduce_fusion.2
  8.4 1.1 multiply_reduce_fusion.5
  9.5 0.7 fusion.61
  10.4 1.0 multiply_convert_fusion.4
  11.5 3.4 multiply_convert_fusion.2
  15.0 0.8 copy-done.5
  15.8 0.4 fusion.63
  16.2 0.2 multiply_reduce_fusion.4
  16.4 0.4 copy-done.13
  16.8 0.1 multiply_convert_fusion.3
  16.9 0.2 fusion.65
  17.4 45.3 %all-gather.1 = bf16[16,1,8448]{2,1,0:T(2,128)(2,1)S(1)} all-gather(bf16[1,1,8448]{2,1,0:T(2,128)(2,1)S(1)} %reshape.176), channel_id=2, replica_groups=mesh['groups'=2,'row'=16,'col'=4,'sub'=2] {'row'}, dimensions={0}, use_global_device_ids=true | all-gather | bytes 287232 | tf_op jit(solution)/shard_map/all_gather | solution.py:27
  62.9 0.7 reshape.192
  63.6 12.2 %all-to-all-start.1 = ((bf16[8,2,256]{2,1,0:T(2,128)(2,1)}), bf16[8,2,256]{2,1,0:T(2,128)(2,1)S(1)}, u32[]{:S(2)}, u32[]{:S(2)}) async-start(bf16[8,2,256]{2,1,0:T(2,128)(2,1)} %reshape.192), calls=%async_computation.1 | async-start | bytes 16384 | tf_op jit(solution)/shard_map/all_to_all | solution.py:130
  76.1 13.7 %all_gather.11 = bf16[64,1056]{1,0:T(8,128)(2,1)S(1)} all-gather(bf16[8,1056]{1,0:T(8,128)(2,1)S(1)} %pad_maximum_fusion.2), channel_id=1, replica_groups=mesh['groups'=2,'row'=16,'col'=4,'sub'=2] {'col','sub'}, dimensions={0}, use_global_device_ids=true | all-gather | bytes 152064 | tf_op jit(solution)/shard_map/all_gather | solution.py:16
  89.8 0.2 copy.60
  90.1 0.9 copy.49
  90.9 4.1 all-to-all-start
  95.1 0.2 fusion.35
  95.3 1.7 multiply_convert_fusion
  97.1 3.2 copy.56
  100.3 1.7 multiply_convert_fusion.1
  102.0 3.2 copy.53
  105.2 3.8 fusion.10
  109.0 1.5 fusion.19
  110.5 0.8 copy.63
  111.2 1.8 convert_element_type.80
  113.1 5.0 all-to-all-start.3
  118.1 1.9 reshape.161
  120.0 1.0 copy.54
  120.9 3.6 fusion.29
  124.6 1.3 fusion.32
  125.9 1.0 copy.76
  126.9 0.8 copy.59
  127.7 1.2 convert_element_type.77
  128.9 4.8 all-to-all-start.2
  133.7 3.2 fusion.1
  136.9 0.1 copy.64
  137.2 0.9 copy.65
  138.0 1.0 all-to-all-done.2
  139.0 4.0 all-to-all-start.4
  143.0 0.3 all-reduce.4.cloned.1.call-start
  143.3 1.2 fusion
  144.5 0.9 copy-done.3
  145.4 2.7 copy.67
  148.2 2.7 copy.70
  150.9 0.9 convolution_bitcast_fusion
  151.9 1.8 fusion.22
  153.8 2.7 all-to-all-done.4
  156.7 0.1 fusion.49
  156.8 0.8 fusion.66
  157.6 0.3 multiply_reduce_fusion
  158.0 0.2 convert_add_fusion
  158.2 1.3 fusion.50
  159.6 2.1 add_convert_fusion
  161.7 1.3 fusion.67
  163.1 0.5 multiply_reduce_fusion.1
  163.6 252.7 %all-reduce = (f32[256]{0:T(256)}, f32[256]{0:T(256)}) all-reduce(f32[256]{0:T(256)S(1)} %get-tuple-element.9, f32[256]{0:T(256)S(1)} %get-tuple-element.7), channel_id=1, replica_groups=mesh['groups'=2,'row'=16,'col'=4,'sub'=2] {'row','col','sub'}, use_global_device_ids=true, to_apply=%region_15.0 | all-reduce | flops 512 | bytes 4096 | tf_op jit(solution)/shard_map/psum | solution.py:199
  416.2 0.9 add_convert_fusion.1
  417.1 95.3 %all-reduce.4.cloned.1.call-done = (f32[1024,128]{1,0:T(8,128)}, f32[256,64]{0,1:T(8,128)}, f32[256,1024]{1,0:T(8,128)}, f32[1024,256]{1,0:T(8,128)}) async-done(((f32[1024,128]{1,0:T(8,128)}, f32[256,64]{0,1:T(8,128)}, f32[256,1024]{1,0:T(8,128)}, f32[1024,256]{1,0:T(8,128)}), (f32[1024,128]{1,0:T(8,128)}, f32[256,64]{0,1:T(8,128)}, f32[256,1024]{1,0:T(8,128)}, ...) | async-done | bytes 2686992 | tf_op jit(solution)/shard_map/psum | solution.py:199
  512.4 1.9 copy.122
  514.2 1.5 copy.123
  515.7 2.3 copy.124
  518.0 2.3 copy.125
  (90 shorter events, 1.9 us)
Async XLA Ops:
  7.2 4.3 copy-start
  8.4 6.6 %copy-start.17 = (f32[256]{0:T(256)}, f32[256]{0:T(256)S(1)}, u32[]{:S(2)}) copy-start(f32[256]{0:T(256)S(1)} %div.30) | copy-start | bytes 3076
  9.5 5.4 %copy-start.19 = (f32[256]{0:T(256)}, f32[256]{0:T(256)S(1)}, u32[]{:S(2)}) copy-start(f32[256]{0:T(256)S(1)} %rsqrt.20) | copy-start | bytes 3076
  10.3 6.7 %copy-start.21 = (f32[256]{0:T(256)}, f32[256]{0:T(256)S(1)}, u32[]{:S(2)}) copy-start(f32[256]{0:T(256)S(1)} %mul.200) | copy-start | bytes 3076
  11.5 4.3 copy-start.4
  11.5 4.3 copy-start.8
  11.5 5.3 copy-start.23
  11.5 5.4 %copy-start.10 = (bf16[256,64]{0,1:T(8,128)(2,1)S(1)}, bf16[256,64]{0,1:T(8,128)(2,1)}, u32[]{:S(2)}) copy-start(bf16[256,64]{0,1:T(8,128)(2,1)} %param.20) | copy-start | bytes 98308
  15.0 0.8 copy-start.5
  16.2 0.6 copy-start.13
  16.8 59.3 %copy-start.15 = (f32[256]{0:T(256)}, f32[256]{0:T(256)S(1)}, u32[]{:S(2)}) copy-start(f32[256]{0:T(256)S(1)} %add_rsqrt_fusion.1) | copy-start | bytes 3076
  63.6 27.3 %all-to-all-start.1 = ((bf16[8,2,256]{2,1,0:T(2,128)(2,1)}), bf16[8,2,256]{2,1,0:T(2,128)(2,1)S(1)}, u32[]{:S(2)}, u32[]{:S(2)}) async-start(bf16[8,2,256]{2,1,0:T(2,128)(2,1)} %reshape.192), calls=%async_computation.1 | async-start | bytes 16384 | tf_op jit(solution)/shard_map/all_to_all | solution.py:130
  90.9 22.1 %all-to-all-start = ((bf16[8,8,2048]{2,0,1:T(8,128)(2,1)}), bf16[8,8,2048]{2,0,1:T(8,128)(2,1)}, u32[]{:S(2)}, u32[]{:S(2)}) async-start(bf16[8,8,2048]{2,0,1:T(8,128)(2,1)} %copy.49), calls=%async_computation | async-start | bytes 524288 | tf_op jit(solution)/shard_map/all_to_all | solution.py:129
  105.2 3.8 copy-start.1
  113.1 15.9 %all-to-all-start.3 = ((bf16[8,8,2048]{2,1,0:T(8,128)(2,1)}), bf16[8,8,2048]{2,1,0:T(8,128)(2,1)S(1)}, u32[]{:S(2)}, u32[]{:S(2)}) async-start(bf16[8,8,2048]{2,1,0:T(8,128)(2,1)} %convert_element_type.80), calls=%async_computation.3 | async-start | bytes 524288 | tf_op jit(solution)/shard_map/all_to_all | solution.py:165
  120.9 3.7 copy-start.2
  128.9 10.1 %all-to-all-start.2 = ((bf16[8,8,1024]{2,1,0:T(8,128)(2,1)}), bf16[8,8,1024]{2,1,0:T(8,128)(2,1)S(1)}, u32[]{:S(2)}, u32[]{:S(2)}) async-start(bf16[8,8,1024]{2,1,0:T(8,128)(2,1)} %convert_element_type.77), calls=%async_computation.2 | async-start | bytes 262144 | tf_op jit(solution)/shard_map/all_to_all | solution.py:43
  139.0 17.5 %all-to-all-start.4 = ((bf16[16,8,1024]{2,1,0:T(8,128)(2,1)}), bf16[16,8,1024]{2,1,0:T(8,128)(2,1)S(1)}, u32[]{:S(2)}, u32[]{:S(2)}) async-start(bf16[16,8,1024]{2,1,0:T(8,128)(2,1)} %copy.65), calls=%async_computation.4 | async-start | bytes 524288 | tf_op jit(solution)/shard_map/all_to_all | solution.py:43
  143.0 369.4 %all-reduce.4.cloned.1.call-start = ((), (), s32[]{:S(2)}) async-start(), calls=%async_computation.5 | async-start | bytes 5373952 | tf_op jit(solution)/shard_map/psum | solution.py:199
  143.3 2.2 copy-start.3
  148.1 2.7 copy-start.7
  151.8 4.8 copy-start.22
  151.8 5.8 %copy-start.11 = (bf16[256,64]{0,1:T(8,128)(2,1)S(1)}, bf16[256,64]{0,1:T(8,128)(2,1)}, u32[]{:S(2)}) copy-start(bf16[256,64]{0,1:T(8,128)(2,1)} %param.20) | copy-start | bytes 98308
  151.8 5.8 %copy-start.14 = (f32[256]{0:T(256)S(1)}, f32[256]{0:T(256)}, u32[]{:S(2)}) copy-start(f32[256]{0:T(256)} %copy-done.13) | copy-start | bytes 3076
  151.8 5.8 %copy-start.16 = (f32[256]{0:T(256)S(1)}, f32[256]{0:T(256)}, u32[]{:S(2)}) copy-start(f32[256]{0:T(256)} %copy-done.15) | copy-start | bytes 3076
  151.9 5.8 %copy-start.24 = (f32[256]{0:T(256)S(1)}, f32[256]{0:T(256)}, u32[]{:S(2)}) copy-start(f32[256]{0:T(256)} %param.19) | copy-start | bytes 3076
  151.9 6.1 %copy-start.12 = (bf16[8,32,256]{2,1,0:T(8,128)(2,1)S(1)}, bf16[8,32,256]{2,1,0:T(8,128)(2,1)}, u32[]{:S(2)}) copy-start(bf16[8,32,256]{2,1,0:T(8,128)(2,1)} %param.15) | copy-start | bytes 393220
  151.9 6.3 %copy-start.6 = (bf16[256,1024]{1,0:T(8,128)(2,1)S(1)}, bf16[256,1024]{1,0:T(8,128)(2,1)}, u32[]{:S(2)}) copy-start(bf16[256,1024]{1,0:T(8,128)(2,1)} %copy-done.5) | copy-start | bytes 1572868
  151.9 7.7 %copy-start.9 = (bf16[1024,256]{1,0:T(8,128)(2,1)S(1)}, bf16[1024,256]{1,0:T(8,128)(2,1)}, u32[]{:S(2)}) copy-start(bf16[1024,256]{1,0:T(8,128)(2,1)} %param.18) | copy-start | bytes 1572868
  159.5 3.5 copy-start.18
  159.5 3.5 copy-start.20
  159.5 3.5 copy-start.25
Sparse Core Ops, SparseCore 0:
  163.2 349.1 all-reduce.3
where the time goes:
time: 528 us; the launch traced here: 527 us
  blocking collectives  312 us (59%)
  waiting for transfers between devices  99 us (19%)
  local copies, waits for them, and re-layouts  34.5 us (7%)
  matrix products  31.3 us (6%)
  starting transfers between devices  30.4 us (6%)
  between operations  14.6 us (3%)
  other arithmetic  5.63 us (1%)
    psum x1, blocking collectives, per_device(): lax.psum((result_adjoint, operand_adjoint, expansion_adjoint, hidden_adjo...  253 us
    psum x1, waiting for transfers between devices, per_device(): lax.psum((result_adjoint, operand_adjoint, expansion_adjoint, hidden_adjo...  95.3 us
    all_gather x1, blocking collectives, one_gather(): lines, at, done = (lax.all_gather(vector, axis), 0, [])  45.3 us
    all_gather x1, blocking collectives, in_one_piece(): lax.all_gather(both, axis, axis=dim, tiled=True)  13.7 us
    all_to_all x1, starting transfers between devices, per_device(): lax.all_to_all(keep_spread, ('col', 'sub'), split_axis=1, concat_axis=0,...  12.2 us
    unnamed x60, local copies, waits for them, and re-layouts  11 us
  transfers between devices with their start and end apart: 6, of which 3 were waited for; matrix products, arithmetic and copies ran while one was open for 9% of the time, Pallas kernels for 0%

commit v1 on v0

--- a/solution.py
+++ b/solution.py
@@ -197,15 +197,18 @@
         normed_input_gradient * feedforward_scale, transition_standardized, transition_inv_deviation
     )
     weight_grads = lax.psum(
-        (
-            result_adjoint,
-            operand_adjoint,
-            expansion_adjoint,
-            hidden_adjoint,
-            feedforward_scale_adjoint,
-            product_scale_adjoint,
-        ),
-        ("row", "col", "sub"),
+        lax.psum(
+            (
+                result_adjoint,
+                operand_adjoint,
+                expansion_adjoint,
+                hidden_adjoint,
+                feedforward_scale_adjoint,
+                product_scale_adjoint,
+            ),
+            ("col", "sub"),
+        ),
+        "row",
     )
     return (
         alignment_start_adjoint.astype(jnp.bfloat16).reshape(

time: 528 us -> 406 us (0.77)
  the two profiles are of different devices: /device:TPU:33 before, /device:TPU:34 now
where the time goes in v1:
time: 406 us; the launch traced here: 405 us
  waiting for transfers between devices  184 us (45%)
  blocking collectives  110 us (27%)
  local copies, waits for them, and re-layouts  35.1 us (9%)
  matrix products  31.3 us (8%)
  starting transfers between devices  24 us (6%)
  between operations  14.6 us (4%)
  other arithmetic  5.63 us (1%)
    psum x1, waiting for transfers between devices, per_device(): lax.psum(lax.psum((result_adjoint, operand_adjoint, expansion_adjoint, hi...  103 us
    psum x1, waiting for transfers between devices, per_device(): lax.psum((result_adjoint, operand_adjoint, expansion_adjoint, hidden_adjo...  73.5 us
    all_gather x1, blocking collectives, one_gather(): lines, at, done = (lax.all_gather(vector, axis), 0, [])  51.4 us
    psum x1, blocking collectives, per_device(): lax.psum(lax.psum((result_adjoint, operand_adjoint, expansion_adjoint, hi...  31.7 us
    psum x1, blocking collectives, per_device(): lax.psum((result_adjoint, operand_adjoint, expansion_adjoint, hidden_adjo...  13.5 us
    all_gather x1, blocking collectives, in_one_piece(): lax.all_gather(both, axis, axis=dim, tiled=True)  12.9 us
    unnamed x60, local copies, waits for them, and re-layouts  11.6 us
    all_to_all x2, starting transfers between devices, sent_and_summed(): lax.all_to_all(parts, axis, split_axis=0, concat_axis=0, tiled=True)  8.79 us
  transfers between devices with their start and end apart: 7, of which 4 were waited for; matrix products, arithmetic and copies ran while one was open for 11% of the time, Pallas kernels for 0%

profile of v1, /device:TPU:34, one launch (start us, length us, event | category | flops | bytes accessed | tf_op | source)
XLA Modules:
  0.0 404.6 jit_solution(7563100260490882166)
XLA Ops:
  7.2 1.1 convert_reduce_fusion.2
  8.4 1.1 multiply_reduce_fusion.5
  9.5 0.7 fusion.61
  10.4 1.0 multiply_convert_fusion.4
  11.5 3.4 multiply_convert_fusion.2
  15.0 0.8 copy-done.5
  15.8 0.4 fusion.63
  16.2 0.2 multiply_reduce_fusion.4
  16.4 0.4 copy-done.13
  16.8 0.6 copy-done.15
  17.5 0.2 fusion.65
  17.9 51.4 %all-gather.1 = bf16[16,1,8448]{2,1,0:T(2,128)(2,1)S(1)} all-gather(bf16[1,1,8448]{2,1,0:T(2,128)(2,1)S(1)} %reshape.176), channel_id=2, replica_groups=mesh['groups'=2,'row'=16,'col'=4,'sub'=2] {'row'}, dimensions={0}, use_global_device_ids=true | all-gather | bytes 287232 | tf_op jit(solution)/shard_map/all_gather | solution.py:27
  69.6 0.7 reshape.192
  70.3 5.0 %all-to-all-start.1 = ((bf16[8,2,256]{2,1,0:T(2,128)(2,1)}), bf16[8,2,256]{2,1,0:T(2,128)(2,1)S(1)}, u32[]{:S(2)}, u32[]{:S(2)}) async-start(bf16[8,2,256]{2,1,0:T(2,128)(2,1)} %reshape.192), calls=%async_computation.1 | async-start | bytes 16384 | tf_op jit(solution)/shard_map/all_to_all | solution.py:130
  75.6 12.9 %all_gather.11 = bf16[64,1056]{1,0:T(8,128)(2,1)S(1)} all-gather(bf16[8,1056]{1,0:T(8,128)(2,1)S(1)} %pad_maximum_fusion.2), channel_id=1, replica_groups=mesh['groups'=2,'row'=16,'col'=4,'sub'=2] {'col','sub'}, dimensions={0}, use_global_device_ids=true | all-gather | bytes 152064 | tf_op jit(solution)/shard_map/all_gather | solution.py:16
  88.6 0.2 copy.60
  88.9 0.9 copy.49
  89.7 4.8 %all-to-all-start = ((bf16[8,8,2048]{2,0,1:T(8,128)(2,1)}), bf16[8,8,2048]{2,0,1:T(8,128)(2,1)}, u32[]{:S(2)}, u32[]{:S(2)}) async-start(bf16[8,8,2048]{2,0,1:T(8,128)(2,1)} %copy.49), calls=%async_computation | async-start | bytes 524288 | tf_op jit(solution)/shard_map/all_to_all | solution.py:129
  94.7 0.2 fusion.35
  94.8 1.7 multiply_convert_fusion
  96.6 3.2 copy.56
  99.8 1.7 multiply_convert_fusion.1
  101.5 3.2 copy.53
  104.7 3.8 fusion.10
  108.5 1.5 fusion.19
  110.0 0.8 copy.63
  110.7 1.8 convert_element_type.80
  112.6 5.0 %all-to-all-start.3 = ((bf16[8,8,2048]{2,1,0:T(8,128)(2,1)}), bf16[8,8,2048]{2,1,0:T(8,128)(2,1)S(1)}, u32[]{:S(2)}, u32[]{:S(2)}) async-start(bf16[8,8,2048]{2,1,0:T(8,128)(2,1)} %convert_element_type.80), calls=%async_computation.3 | async-start | bytes 524288 | tf_op jit(solution)/shard_map/all_to_all | solution.py:165
  117.6 1.9 reshape.161
  119.5 1.0 copy.54
  120.5 3.6 fusion.29
  124.1 1.3 fusion.32
  125.4 1.0 copy.76
  126.5 0.8 copy.59
  127.3 1.2 convert_element_type.77
  128.4 4.8 %all-to-all-start.2 = ((bf16[8,8,1024]{2,1,0:T(8,128)(2,1)}), bf16[8,8,1024]{2,1,0:T(8,128)(2,1)S(1)}, u32[]{:S(2)}, u32[]{:S(2)}) async-start(bf16[8,8,1024]{2,1,0:T(8,128)(2,1)} %convert_element_type.77), calls=%async_computation.2 | async-start | bytes 262144 | tf_op jit(solution)/shard_map/all_to_all | solution.py:43
  133.3 3.2 fusion.1
  136.7 0.9 copy.65
  137.5 0.4 all-to-all-done.2
  137.9 4.0 all-to-all-start.4
  141.9 0.3 all-reduce.9.cloned.1.call-start
  142.2 1.2 fusion
  143.4 0.9 copy-done.3
  144.4 2.7 copy.67
  147.1 2.7 copy.70
  149.8 0.9 convolution_bitcast_fusion
  150.8 1.8 fusion.22
  152.7 6.9 %all-to-all-done.4 = bf16[16,8,1024]{2,1,0:T(8,128)(2,1)S(1)} async-done(((bf16[16,8,1024]{2,1,0:T(8,128)(2,1)}), bf16[16,8,1024]{2,1,0:T(8,128)(2,1)S(1)}, u32[]{:S(2)}, u32[]{:S(2)}) %all-to-all-start.4) | async-done | bytes 262176 | tf_op jit(solution)/shard_map/all_to_all | solution.py:43
  159.9 0.8 fusion.66
  160.7 0.3 multiply_reduce_fusion
  161.1 0.2 convert_add_fusion
  161.3 1.3 fusion.50
  162.6 2.1 add_convert_fusion
  164.8 1.3 fusion.67
  166.2 73.5 %all-reduce.9.cloned.1.call-done = (f32[1024,128]{1,0:T(8,128)}, f32[256,64]{0,1:T(8,128)}, f32[256,1024]{1,0:T(8,128)}, f32[1024,256]{1,0:T(8,128)}) async-done(((f32[1024,128]{1,0:T(8,128)}, f32[256,64]{0,1:T(8,128)}, f32[256,1024]{1,0:T(8,128)}, f32[1024,256]{1,0:T(8,128)}), (f32[1024,128]{1,0:T(8,128)}, f32[256,64]{0,1:T(8,128)}, f32[256,1024]{1,0:T(8,128)}, ...) | async-done | bytes 2686992 | tf_op jit(solution)/shard_map/psum | solution.py:200
  239.9 0.5 multiply_reduce_fusion.1
  240.3 13.5 %all-reduce.2 = (f32[256]{0:T(256)S(1)}, f32[256]{0:T(256)S(1)}) all-reduce(f32[256]{0:T(256)S(1)} %get-tuple-element.9, f32[256]{0:T(256)S(1)} %get-tuple-element.7), channel_id=1, replica_groups=mesh['groups'=2,'row'=16,'col'=4,'sub'=2] {'col','sub'}, use_global_device_ids=true, to_apply=%region_19.0 | all-reduce | flops 512 | bytes 4096 | tf_op jit(solution)/shard_map/psum | solution.py:200
  253.8 31.7 %all-reduce = (f32[256]{0:T(256)}, f32[256]{0:T(256)}) all-reduce(f32[256]{0:T(256)S(1)} %get-tuple-element.19, f32[256]{0:T(256)S(1)} %get-tuple-element.20), channel_id=1, replica_groups=mesh['groups'=2,'row'=16,'col'=4,'sub'=2] {'row'}, use_global_device_ids=true, to_apply=%region_20.0 | all-reduce | flops 512 | bytes 4096 | tf_op jit(solution)/shard_map/psum | solution.py:199
  285.5 0.9 add_convert_fusion.1
  286.4 103.5 %all-reduce.7.cloned.1.call-done = (f32[1024,128]{1,0:T(8,128)}, f32[256,64]{0,1:T(8,128)}, f32[256,1024]{1,0:T(8,128)}, f32[1024,256]{1,0:T(8,128)}) async-done(((f32[1024,128]{1,0:T(8,128)}, f32[256,64]{0,1:T(8,128)}, f32[256,1024]{1,0:T(8,128)}, f32[1024,256]{1,0:T(8,128)}), (f32[1024,128]{1,0:T(8,128)}, f32[256,64]{0,1:T(8,128)}, f32[256,1024]{1,0:T(8,128)}, ...) | async-done | bytes 2686992 | tf_op jit(solution)/shard_map/psum | solution.py:199
  389.9 1.9 copy.126
  391.8 1.5 copy.127
  393.2 2.3 copy.128
  395.5 2.3 copy.129
  (94 shorter events, 2.5 us)
Async XLA Ops:
  7.2 4.3 %copy-start = (bf16[256,1024]{1,0:T(8,128)(2,1)S(1)}, bf16[256,1024]{1,0:T(8,128)(2,1)}, u32[]{:S(2)}) copy-start(bf16[256,1024]{1,0:T(8,128)(2,1)} %param.17) | copy-start | bytes 1572868
  8.4 2.1 copy-start.17
  9.5 0.9 copy-start.19
  10.3 7.3 %copy-start.21 = (f32[256]{0:T(256)}, f32[256]{0:T(256)S(1)}, u32[]{:S(2)}) copy-start(f32[256]{0:T(256)S(1)} %mul.200) | copy-start | bytes 3076
  11.5 4.3 %copy-start.4 = (bf16[8,32,256]{2,1,0:T(8,128)(2,1)S(1)}, bf16[8,32,256]{2,1,0:T(8,128)(2,1)}, u32[]{:S(2)}) copy-start(bf16[8,32,256]{2,1,0:T(8,128)(2,1)} %param.11) | copy-start | bytes 393220
  11.5 4.3 %copy-start.8 = (bf16[1024,256]{1,0:T(8,128)(2,1)S(1)}, bf16[1024,256]{1,0:T(8,128)(2,1)}, u32[]{:S(2)}) copy-start(bf16[1024,256]{1,0:T(8,128)(2,1)} %param.18) | copy-start | bytes 1572868
  11.5 5.8 %copy-start.23 = (f32[256]{0:T(256)S(1)}, f32[256]{0:T(256)}, u32[]{:S(2)}) copy-start(f32[256]{0:T(256)} %param.19) | copy-start | bytes 3076
  11.5 5.9 %copy-start.10 = (bf16[256,64]{0,1:T(8,128)(2,1)S(1)}, bf16[256,64]{0,1:T(8,128)(2,1)}, u32[]{:S(2)}) copy-start(bf16[256,64]{0,1:T(8,128)(2,1)} %param.20) | copy-start | bytes 98308
  15.0 0.8 copy-start.5
  16.2 0.6 copy-start.13
  16.8 0.6 copy-start.15
  70.3 19.4 %all-to-all-start.1 = ((bf16[8,2,256]{2,1,0:T(2,128)(2,1)}), bf16[8,2,256]{2,1,0:T(2,128)(2,1)S(1)}, u32[]{:S(2)}, u32[]{:S(2)}) async-start(bf16[8,2,256]{2,1,0:T(2,128)(2,1)} %reshape.192), calls=%async_computation.1 | async-start | bytes 16384 | tf_op jit(solution)/shard_map/all_to_all | solution.py:130
  89.7 22.8 %all-to-all-start = ((bf16[8,8,2048]{2,0,1:T(8,128)(2,1)}), bf16[8,8,2048]{2,0,1:T(8,128)(2,1)}, u32[]{:S(2)}, u32[]{:S(2)}) async-start(bf16[8,8,2048]{2,0,1:T(8,128)(2,1)} %copy.49), calls=%async_computation | async-start | bytes 524288 | tf_op jit(solution)/shard_map/all_to_all | solution.py:129
  104.7 3.8 copy-start.1
  112.6 15.9 %all-to-all-start.3 = ((bf16[8,8,2048]{2,1,0:T(8,128)(2,1)}), bf16[8,8,2048]{2,1,0:T(8,128)(2,1)S(1)}, u32[]{:S(2)}, u32[]{:S(2)}) async-start(bf16[8,8,2048]{2,1,0:T(8,128)(2,1)} %convert_element_type.80), calls=%async_computation.3 | async-start | bytes 524288 | tf_op jit(solution)/shard_map/all_to_all | solution.py:165
  120.4 3.7 copy-start.2
  128.4 9.5 %all-to-all-start.2 = ((bf16[8,8,1024]{2,1,0:T(8,128)(2,1)}), bf16[8,8,1024]{2,1,0:T(8,128)(2,1)S(1)}, u32[]{:S(2)}, u32[]{:S(2)}) async-start(bf16[8,8,1024]{2,1,0:T(8,128)(2,1)} %convert_element_type.77), calls=%async_computation.2 | async-start | bytes 262144 | tf_op jit(solution)/shard_map/all_to_all | solution.py:43
  137.9 21.7 %all-to-all-start.4 = ((bf16[16,8,1024]{2,1,0:T(8,128)(2,1)}), bf16[16,8,1024]{2,1,0:T(8,128)(2,1)S(1)}, u32[]{:S(2)}, u32[]{:S(2)}) async-start(bf16[16,8,1024]{2,1,0:T(8,128)(2,1)} %copy.65), calls=%async_computation.4 | async-start | bytes 524288 | tf_op jit(solution)/shard_map/all_to_all | solution.py:43
  141.9 97.9 %all-reduce.9.cloned.1.call-start = ((), (), s32[]{:S(2)}) async-start(), calls=%async_computation.6 | async-start | bytes 5373952 | tf_op jit(solution)/shard_map/psum | solution.py:200
  142.2 2.2 copy-start.3
  147.1 2.7 copy-start.7
  150.7 9.0 %copy-start.22 = (f32[256]{0:T(256)S(1)}, f32[256]{0:T(256)}, u32[]{:S(2)}) copy-start(f32[256]{0:T(256)} %copy-done.21) | copy-start | bytes 3076
  150.7 10.0 %copy-start.11 = (bf16[256,64]{0,1:T(8,128)(2,1)S(1)}, bf16[256,64]{0,1:T(8,128)(2,1)}, u32[]{:S(2)}) copy-start(bf16[256,64]{0,1:T(8,128)(2,1)} %param.20) | copy-start | bytes 98308
  150.8 10.0 %copy-start.14 = (f32[256]{0:T(256)S(1)}, f32[256]{0:T(256)}, u32[]{:S(2)}) copy-start(f32[256]{0:T(256)} %copy-done.13) | copy-start | bytes 3076
  150.8 10.0 %copy-start.16 = (f32[256]{0:T(256)S(1)}, f32[256]{0:T(256)}, u32[]{:S(2)}) copy-start(f32[256]{0:T(256)} %copy-done.15) | copy-start | bytes 3076
  150.8 9.9 %copy-start.24 = (f32[256]{0:T(256)S(1)}, f32[256]{0:T(256)}, u32[]{:S(2)}) copy-start(f32[256]{0:T(256)} %param.19) | copy-start | bytes 3076
  150.8 10.3 %copy-start.12 = (bf16[8,32,256]{2,1,0:T(8,128)(2,1)S(1)}, bf16[8,32,256]{2,1,0:T(8,128)(2,1)}, u32[]{:S(2)}) copy-start(bf16[8,32,256]{2,1,0:T(8,128)(2,1)} %param.15) | copy-start | bytes 393220
  150.8 10.5 %copy-start.6 = (bf16[256,1024]{1,0:T(8,128)(2,1)S(1)}, bf16[256,1024]{1,0:T(8,128)(2,1)}, u32[]{:S(2)}) copy-start(bf16[256,1024]{1,0:T(8,128)(2,1)} %copy-done.5) | copy-start | bytes 1572868
  150.8 11.8 %copy-start.9 = (bf16[1024,256]{1,0:T(8,128)(2,1)S(1)}, bf16[1024,256]{1,0:T(8,128)(2,1)}, u32[]{:S(2)}) copy-start(bf16[1024,256]{1,0:T(8,128)(2,1)} %param.18) | copy-start | bytes 1572868
  164.8 75.1 %copy-start.18 = (f32[256]{0:T(256)S(1)}, f32[256]{0:T(256)}, u32[]{:S(2)}) copy-start(f32[256]{0:T(256)} %copy-done.17) | copy-start | bytes 3076
  164.8 75.1 %copy-start.20 = (f32[256]{0:T(256)S(1)}, f32[256]{0:T(256)}, u32[]{:S(2)}) copy-start(f32[256]{0:T(256)} %copy-done.19) | copy-start | bytes 3076
  164.8 75.1 %copy-start.25 = (f32[256]{0:T(256)S(1)}, f32[256]{0:T(256)}, u32[]{:S(2)}) copy-start(f32[256]{0:T(256)} %param.16) | copy-start | bytes 3076
  166.2 223.7 %all-reduce.7.cloned.1.call-start = ((), (), s32[]{:S(2)}) async-start(), calls=%async_computation.5 | async-start | bytes 5373952 | tf_op jit(solution)/shard_map/psum | solution.py:199
Sparse Core Ops, SparseCore 0:
  166.3 73.4 all-reduce.8
  242.4 147.4 all-reduce.6
